TPU v7x, 32 devices: a whole 2x2x4 slice. The times are simulated.
32 devices in a mesh: dp: 8 (over z, x), tensor: 4 (over y, core).
Axes of the slice: x: 2, y: 2, z: 4, core: 2. Of those that a mesh axis runs over, the one named last changes fastest.
Arguments:
- hidden: bfloat16 [2048, 14336], P('dp', 'tensor'), parts along dimension 0, may hold values from -16 to 16
- signs: int32 [14336], P('tensor'), may hold values 0 or 1
- packed: int32 [14336, 512], P('tensor'), may hold values from -2147483648 to 2147483646
- group_scales: int32 [112, 4096], P('tensor'), may hold values from 1 to 16
- residual: bfloat16 [2048, 4096], P(('dp', 'tensor')), parts along dimension 0, may hold values from -16 to 16
Outputs:
- new_residual: bfloat16 [2048, 4096], P(('dp', 'tensor')), parts along dimension 0
- normed: bfloat16 [2048, 4096], P(('dp', 'tensor')), parts along dimension 0
There are 8 independent parts, one for each index of `dp`. A program takes and returns all parts, laid end to end along the dimension named above; an argument that names none is the same for every part. Nothing has to cross between parts.
Inputs may be any that keep to these rules, and one draw needn't show every extreme that they name: `packed`: bits 4 k to 4 k + 3 of word j in row f hold the code of output feature k * 512 + j plus 8.
All inputs are finite; a program needn't handle non-finite values. No bound on the sum of `signs` on one device may be relied on, other than what follows from the above.
Results may differ from a plain program's by a relative error of at most 0.0054.
Values may be sent and summed in bfloat16 or wider, within the bound.
A program may use at most 256 MiB of HBM per device.

v0:
```python
import math

import jax
import jax.numpy as jnp
import numpy as np
from jax import lax
from jax.sharding import PartitionSpec as P

FF = 14336


def paley_table():
    offsets = (np.arange(13)[None, :] - np.arange(13)[:, None]) % 13
    residues = np.zeros(13)
    residues[np.arange(1, 13) ** 2 % 13] = 1.0
    quadratic = np.where(offsets == 0, 0.0, np.where(residues[offsets] > 0, 1.0, -1.0))
    conference = np.zeros((14, 14))
    conference[0, 1:] = 1.0
    conference[1:, 0] = 1.0
    conference[1:, 1:] = quadratic
    upper = np.array([[1.0, 1.0], [1.0, -1.0]])
    lower = np.array([[1.0, -1.0], [-1.0, -1.0]])
    return np.kron(conference, upper) + np.kron(np.eye(14), lower)


def sylvester(order):
    first = lax.broadcasted_iota(jnp.int32, (order, order), 0)
    second = lax.broadcasted_iota(jnp.int32, (order, order), 1)
    common = first & second
    parity = jnp.zeros((order, order), jnp.int32)
    for bit in range(max(order.bit_length() - 1, 0)):
        parity = parity ^ jnp.right_shift(common, bit) & 1
    return (1 - 2 * parity).astype(jnp.float32)


def dequantize(packed, group_scales, local_width):
    word_cols = packed.shape[1]
    group_count = group_scales.shape[0]
    group_size = local_width // group_count
    pieces = []
    for nibble in range(8):
        codes = (jnp.right_shift(packed, 4 * nibble) & 15) - 8
        scales = group_scales[:, nibble * word_cols : (nibble + 1) * word_cols]
        weights = codes.reshape(group_count, group_size, word_cols) * scales[:, None, :]
        pieces.append(weights.reshape(local_width, word_cols).astype(jnp.bfloat16))
    return jnp.concatenate(pieces, axis=1)


def local(hidden, signs, packed, group_scales, residual):
    groups = lax.axis_size("tensor")
    local_width = hidden.shape[1]
    inner = jnp.asarray(paley_table(), jnp.float32)
    outer = sylvester(local_width // 28)
    table = (
        (outer[:, None, :, None] * inner[None, :, None, :])
        .reshape(local_width, local_width)
        .astype(jnp.bfloat16)
    )
    flips = (2 * signs - 1).astype(jnp.bfloat16)
    signed = hidden * flips[None, :]
    partial_rot = jnp.dot(signed, table, preferred_element_type=jnp.float32)
    unit = 1.0 / math.sqrt(FF)
    spread = lax.all_to_all(partial_rot, "tensor", split_axis=0, concat_axis=1, tiled=True)
    token_rows = spread.shape[0]
    stacked = spread.reshape(token_rows, groups, local_width)
    mixed = jnp.einsum("rpw,qp->rqw", stacked, sylvester(groups), precision=lax.Precision.HIGHEST)
    folded = (mixed * unit).astype(jnp.bfloat16).reshape(token_rows, groups * local_width)
    rotated = lax.all_to_all(folded, "tensor", split_axis=1, concat_axis=0, tiled=True)
    weights = dequantize(packed, group_scales, local_width)
    summed = lax.psum_scatter(
        jnp.dot(rotated, weights, preferred_element_type=jnp.float32),
        "tensor",
        scatter_dimension=0,
        tiled=True,
    )
    branch = summed * (1.0 / (45.0 * math.sqrt(FF)))
    new_residual = (residual.astype(jnp.float32) + branch).astype(jnp.bfloat16)
    values = new_residual.astype(jnp.float32)
    normed = values * lax.rsqrt(jnp.mean(values * values, axis=1, keepdims=True) + 1e-05)
    return (new_residual, normed.astype(jnp.bfloat16))


def solution(mesh):
    return jax.shard_map(
        local,
        mesh=mesh,
        in_specs=(
            P("dp", "tensor"),
            P("tensor"),
            P("tensor", None),
            P("tensor", None),
            P(("dp", "tensor"), None),
        ),
        out_specs=(P(("dp", "tensor"), None), P(("dp", "tensor"), None)),
        check_vma=False,
    )
```

profile of v0, /device:TPU:0, one launch (start us, length us, event | category | flops | bytes accessed | tf_op | source)
XLA Modules:
  0.0 432.5 jit_solution(5073815844837032405)
XLA Ops:
  7.2 0.7 add_convert_fusion.1
  8.0 37.3 %multiply_convert_fusion = bf16[128,28,128,28]{3,2,1,0:T(8,128)(2,1)} fusion(f32[28,28]{1,0:T(8,128)} %constant.59.clone, f32[128,128]{1,0:T(8,128)S(1)} %subtract_convert_fusion), kind=kLoop, calls=%fused_computation | loop fusion | flops 25690112 | bytes 25758784 | tf_op jit(solution)/shard_map/convert_element_type | solution.py:57
  45.3 214.7 %reshape.100 = bf16[3584,3584,1]{1,0,2:T(8,128)(2,1)} reshape(bf16[128,28,128,28]{3,2,1,0:T(8,128)(2,1)} %multiply_convert_fusion) | data formatting | bytes 51380224 | tf_op jit(solution)/shard_map/convert_element_type | solution.py:57
  260.2 13.6 %fusion.33 = f32[4,64,3584]{2,1,0:T(8,128)} fusion(bf16[4,64,3584]{2,1,0:T(8,128)(2,1)S(1)} %bitcast.51, bf16[3584,3584,1]{1,0,2:T(8,128)(2,1)} %reshape.100), kind=kOutput, calls=%fused_computation.58 | convolution fusion | flops 6576668672 | bytes 31195136 | tf_op jit(solution)/shard_map/dot_general | solution.py:61
  273.8 5.1 %all-to-all-start = ((f32[4,64,3584]{2,1,0:T(8,128)}), f32[4,64,3584]{2,1,0:T(8,128)}, u32[]{:S(2)}, u32[]{:S(2)}) async-start(f32[4,64,3584]{2,1,0:T(8,128)} %fusion.33), calls=%async_computation | async-start | bytes 7340032 | tf_op jit(solution)/shard_map/all_to_all | solution.py:63
  278.9 14.1 %fusion = (bf16[3584,512]{1,0:T(8,128)(2,1)}, bf16[3584,512]{1,0:T(8,128)(2,1)}, bf16[3584,512]{1,0:T(8,128)(2,1)S(1)}, bf16[3584,512]{1,0:T(8,128)(2,1)S(1)}, b...) fusion(s32[3584,512]{1,0:T(8,128)} %param.8, ...), kind=kLoop, calls=%fused_computation.2 | loop fusion | flops 73400320 | bytes 37158912 | tf_op jit(solution)/shard_map/convert_element_type | solution.py:45
  293.1 2.1 constant_dynamic-update-slice_fusion.7
  295.2 2.1 constant_dynamic-update-slice_fusion.6
  297.3 2.1 constant_dynamic-update-slice_fusion.5
  299.4 2.1 constant_dynamic-update-slice_fusion.4
  301.5 2.1 constant_dynamic-update-slice_fusion.3
  303.6 18.6 %all-to-all-done = f32[4,64,3584]{2,1,0:T(8,128)} async-done(((f32[4,64,3584]{2,1,0:T(8,128)}), f32[4,64,3584]{2,1,0:T(8,128)}, u32[]{:S(2)}, u32[]{:S(2)}) %all-to-all-start) | async-done | bytes 3670048 | tf_op jit(solution)/shard_map/all_to_all | solution.py:63
  322.2 11.6 %fusion.9 = bf16[64,4,3584]{2,1,0:T(4,128)(2,1)S(1)} fusion(f32[4,64,3584]{2,1,0:T(8,128)} %all-to-all-done), kind=kOutput, calls=%fused_computation.19 | convolution fusion | flops 45875344 | bytes 5505024 | tf_op jit(solution)/shard_map/rpw,qp->rqw/dot_general | solution.py:66
  333.8 1.6 copy.10
  335.4 3.6 all-to-all-start.1
  339.0 0.3 reduce-scatter.2.cloned.1.call-start
  339.3 4.3 constant_dynamic-update-slice_fusion.2
  343.6 2.1 constant_dynamic-update-slice_fusion.1
  345.7 2.1 constant_dynamic-update-slice_fusion
  347.8 14.0 %all-to-all-done.1 = bf16[64,4,3584]{2,0,1:T(8,128)(2,1)S(1)} async-done(((bf16[64,4,3584]{2,0,1:T(8,128)(2,1)}), bf16[64,4,3584]{2,0,1:T(8,128)(2,1)S(1)}, u32[]{:S(2)}, u32[]{:S(2)}) %all-to-all-start.1) | async-done | bytes 1835040 | tf_op jit(solution)/shard_map/all_to_all | solution.py:68
  361.8 15.6 %fusion.34 = f32[256,4096]{1,0:T(8,128)} fusion(bf16[256,3584]{1,0:T(8,128)(2,1)S(1)} %bitcast.50, bf16[3584,4096]{1,0:T(8,128)(2,1)} %constant_dynamic-update-slice_fusion), kind=kOutput, calls=%fused_computation.59 | convolution fusion | flops 7516192768 | bytes 35389440 | tf_op jit(solution)/shard_map/dot_general | solution.py:71
  377.5 45.6 %reduce-scatter.2.cloned.1.call-done = f32[64,4096]{1,0:T(8,128)} async-done(((f32[256,4096]{1,0:T(8,128)}), f32[64,4096]{1,0:T(8,128)}) %reduce-scatter.2.cloned.1.call-update) | async-done | bytes 1048592 | tf_op jit(solution)/shard_map/reduce_scatter | solution.py:70
  423.1 1.5 fusion.12
  424.7 0.9 fusion.13
  (17 shorter events, 0.3 us)
Async XLA Ops:
  45.3 214.7 %copy-start.3 = (bf16[256,3584]{1,0:T(8,128)(2,1)S(1)}, bf16[256,3584]{1,0:T(8,128)(2,1)}, u32[]{:S(2)}) copy-start(bf16[256,3584]{1,0:T(8,128)(2,1)} %param.6) | copy-start | bytes 5505028
  273.8 5.1 %copy-start.5 = (s32[28,4096]{1,0:T(8,128)S(1)}, s32[28,4096]{1,0:T(8,128)}, u32[]{:S(2)}) copy-start(s32[28,4096]{1,0:T(8,128)} %param.9) | copy-start | bytes 1376260
  273.8 48.4 %all-to-all-start = ((f32[4,64,3584]{2,1,0:T(8,128)}), f32[4,64,3584]{2,1,0:T(8,128)}, u32[]{:S(2)}, u32[]{:S(2)}) async-start(f32[4,64,3584]{2,1,0:T(8,128)} %fusion.33), calls=%async_computation | async-start | bytes 7340032 | tf_op jit(solution)/shard_map/all_to_all | solution.py:63
  335.4 26.4 %all-to-all-start.1 = ((bf16[64,4,3584]{2,0,1:T(8,128)(2,1)}), bf16[64,4,3584]{2,0,1:T(8,128)(2,1)S(1)}, u32[]{:S(2)}, u32[]{:S(2)}) async-start(bf16[64,4,3584]{2,0,1:T(8,128)(2,1)} %copy.10), calls=%async_computation.1 | async-start | bytes 3670016 | tf_op jit(solution)/shard_map/all_to_all | solution.py:68
  339.0 84.1 %reduce-scatter.2.cloned.1.call-start = ((), (), s32[]{:S(2)}) async-start(), calls=%async_computation.3 | async-start | bytes 5242880 | tf_op jit(solution)/shard_map/reduce_scatter | solution.py:70
  339.3 4.3 %copy-start.1 = (bf16[3584,512]{1,0:T(8,128)(2,1)S(1)}, bf16[3584,512]{1,0:T(8,128)(2,1)}, u32[]{:S(2)}) copy-start(bf16[3584,512]{1,0:T(8,128)(2,1)} %get-tuple-element.11) | copy-start | bytes 11010052
  339.3 6.4 %copy-start = (bf16[3584,512]{1,0:T(8,128)(2,1)S(1)}, bf16[3584,512]{1,0:T(8,128)(2,1)}, u32[]{:S(2)}) copy-start(bf16[3584,512]{1,0:T(8,128)(2,1)} %get-tuple-element.4) | copy-start | bytes 11010052
  361.8 61.3 %copy-start.4 = (bf16[64,4096]{1,0:T(8,128)(2,1)S(1)}, bf16[64,4096]{1,0:T(8,128)(2,1)}, u32[]{:S(2)}) copy-start(bf16[64,4096]{1,0:T(8,128)(2,1)} %param.10) | copy-start | bytes 1572868
  424.6 1.0 copy-start.2
Sparse Core Ops, SparseCore 0:
  377.6 45.4 reduce-scatter.1
where the time goes:
time: 433 us; the launch traced here: 432 us
  local copies, waits for them, and re-layouts  235 us (54%)
  waiting for transfers between devices  78.3 us (18%)
  other arithmetic  54.8 us (13%)
  matrix products  40.9 us (9%)
  between operations  14.1 us (3%)
  starting transfers between devices  8.93 us (2%)
    convert_element_type x1, local copies, waits for them, and re-layouts, local(): table = (outer[:, None, :, None] * inner[None, :, None, :]).reshape(local...  215 us
    reduce_scatter x1, waiting for transfers between devices, local(): lax.psum_scatter(jnp.dot(rotated, weights, preferred_element_type=jnp.flo...  45.6 us
    convert_element_type x1, other arithmetic, local(): table = (outer[:, None, :, None] * inner[None, :, None, :]).reshape(local...  37.3 us
    all_to_all x1, waiting for transfers between devices, local(): lax.all_to_all(partial_rot, 'tensor', split_axis=0, concat_axis=1, tiled=...  18.6 us
    unnamed x19, local copies, waits for them, and re-layouts  17 us
    dot_general x1, matrix products, local(): jnp.dot(rotated, weights, preferred_element_type=jnp.float32)  15.6 us
    convert_element_type x1, other arithmetic, dequantize(): pieces.append(weights.reshape(local_width, word_cols).astype(jnp.bfloat16))  14.1 us
    all_to_all x1, waiting for transfers between devices, local(): lax.all_to_all(folded, 'tensor', split_axis=1, concat_axis=0, tiled=True)  14 us
  transfers between devices with their start and end apart: 3, of which 3 were waited for; matrix products, arithmetic and copies ran while one was open for 8% of the time, Pallas kernels for 0%

commit v1 on v0

v1 whole, which is shorter than its diff:
```python
import functools
import math

import jax
import jax.numpy as jnp
import ml_dtypes
import numpy as np
from jax import lax
from jax.experimental import pallas as pl
from jax.experimental.pallas import tpu as pltpu
from jax.sharding import PartitionSpec as P

PALEY = 28
LANES = 128
NIBBLES = 8
SLAB = 16
MESH = pl.DeviceIdType.MESH


def paley_table():
    offsets = (np.arange(13)[None, :] - np.arange(13)[:, None]) % 13
    residues = np.zeros(13)
    residues[np.arange(1, 13) ** 2 % 13] = 1.0
    quadratic = np.where(offsets == 0, 0.0, np.where(residues[offsets] > 0, 1.0, -1.0))
    conference = np.zeros((14, 14))
    conference[0, 1:] = 1.0
    conference[1:, 0] = 1.0
    conference[1:, 1:] = quadratic
    upper = np.array([[1.0, 1.0], [1.0, -1.0]])
    lower = np.array([[1.0, -1.0], [-1.0, -1.0]])
    return np.kron(conference, upper) + np.kron(np.eye(14), lower)


def sylvester(order):
    table = np.ones((1, 1))
    while table.shape[0] < order:
        table = np.kron(np.array([[1.0, 1.0], [1.0, -1.0]]), table)
    return table


def parity_sign(index, other, bits):
    common = index & other
    parity = common & 1
    for bit in range(1, bits):
        parity = parity ^ ((common >> bit) & 1)
    return (1 - 2 * parity).astype(jnp.float32)


def kernel(
    groups,
    signed,
    packed,
    scales,
    table,
    residual,
    new_residual,
    normed,
    words,
    inner,
    gathered,
    scale_f32,
    weights,
    rotated,
    sums,
    own,
    core_out,
    core_in,
    chip_out,
    chip_in,
    word_sem,
    inner_sem,
    self_sem,
    peer_send,
    peer_recv,
    core_send,
    core_recv,
    fold_send,
    fold_recv,
    chip_send,
    chip_recv,
):
    me = lax.axis_index("tensor")
    chips = groups // 2
    chip, core = me // 2, lax.rem(me, 2)
    partner = chip * 2 + 1 - core
    rows, width = signed.shape
    part = rows // groups
    group_count = scales.shape[0]
    group_size = width // group_count
    word_cols = packed.shape[1]
    block = table.shape[0]
    blocks = width // block
    bits = max(groups.bit_length() - 1, 1)

    word_copies = [
        pltpu.make_async_copy(packed, words, word_sem),
        pltpu.make_async_copy(table, inner, inner_sem),
        pltpu.make_async_copy(signed, gathered.at[me], self_sem),
    ]
    for copy in word_copies:
        copy.start()

    def peer(step):
        return lax.rem(chip + step, chips) * 2 + core

    barrier = pltpu.get_barrier_semaphore()
    pl.semaphore_signal(barrier, inc=1, device_id={"tensor": partner}, device_id_type=MESH)
    for step in range(1, chips):
        pl.semaphore_signal(barrier, inc=1, device_id={"tensor": peer(step)}, device_id_type=MESH)
    pl.semaphore_wait(barrier, chips)

    def band(index):
        return pl.ds(pl.multiple_of(index * part, part), part)

    def peer_copy(step, piece):
        return pltpu.make_async_remote_copy(
            src_ref=signed.at[band(piece)],
            dst_ref=gathered.at[me, band(piece)],
            send_sem=peer_send.at[step, piece],
            recv_sem=peer_recv.at[step, piece],
            device_id={"tensor": peer(step)},
            device_id_type=MESH,
        )

    def core_copy(step, piece):
        source = signed.at[band(piece)] if step == 0 else gathered.at[peer(chips - step), band(piece)]
        slot = me if step == 0 else peer(chips - step)
        return pltpu.make_async_remote_copy(
            src_ref=source,
            dst_ref=gathered.at[slot, band(piece)],
            send_sem=core_send.at[step, piece],
            recv_sem=core_recv.at[step, piece],
            device_id={"tensor": partner},
            device_id_type=MESH,
        )

    for piece in range(groups):
        for step in range(1, chips):
            peer_copy(step, piece).start()
        core_copy(0, piece).start()

    scale_f32[...] = scales[...].astype(jnp.float32)
    word_copies[0].wait()

    def dequantize(index, carry):
        start = pl.multiple_of(index * SLAB, SLAB)
        group = index // (group_size // SLAB)
        values = words[pl.ds(start, SLAB), :] ^ jnp.int32(-2004318072)
        for nibble in range(NIBBLES):
            codes = lax.shift_right_arithmetic(lax.shift_left(values, 28 - 4 * nibble), 28)
            scale = scale_f32[pl.ds(group, 1), nibble * word_cols : (nibble + 1) * word_cols]
            weights[nibble, pl.ds(start, SLAB), :] = (codes.astype(jnp.float32) * scale).astype(jnp.bfloat16)
        return carry

    lax.fori_loop(0, width // SLAB, dequantize, 0)
    word_copies[1].wait()
    word_copies[2].wait()

    unit = 1.0 / math.sqrt(groups * width)
    outer = sylvester(blocks)

    def rotate(piece, carry):
        for step in range(1, chips):
            peer_copy(step, piece).wait_recv()
            core_copy(step, piece).start()
        for step in range(chips):
            core_copy(step, piece).wait_recv()
        mixed = []
        for place in range(blocks):
            total = jnp.zeros((part, block), jnp.float32)
            for device in range(groups):
                sign = parity_sign(me, device, bits)
                total += gathered[device, band(piece), place * block : (place + 1) * block].astype(jnp.float32) * sign
            high = total.astype(jnp.bfloat16)
            low = (total - high.astype(jnp.float32)).astype(jnp.bfloat16)
            both = jnp.dot(jnp.concatenate([high, low], axis=0), inner[...], preferred_element_type=jnp.float32)
            mixed.append(both[:part] + both[part:])
        stride = 1
        while stride < blocks:
            for low_index in range(blocks):
                if low_index & stride == 0:
                    first, second = mixed[low_index], mixed[low_index + stride]
                    mixed[low_index], mixed[low_index + stride] = first + second, first - second
            stride *= 2
        for place in range(blocks):
            rotated[band(piece), place * block : (place + 1) * block] = (mixed[place] * unit).astype(jnp.bfloat16)
        return carry

    lax.fori_loop(0, groups, rotate, 0)

    def fold_copy(column):
        return pltpu.make_async_remote_copy(
            src_ref=core_out.at[column],
            dst_ref=core_in.at[column],
            send_sem=fold_send.at[column],
            recv_sem=fold_recv.at[column],
            device_id={"tensor": partner},
            device_id_type=MESH,
        )

    def chip_copy(step, column):
        return pltpu.make_async_remote_copy(
            src_ref=chip_out.at[column, step],
            dst_ref=chip_in.at[column, step],
            send_sem=chip_send.at[step, column],
            recv_sem=chip_recv.at[step, column],
            device_id={"tensor": peer(step)},
            device_id_type=MESH,
        )

    def multiply(column):
        sums[...] = jnp.dot(rotated[...], weights[column], preferred_element_type=jnp.float32)
        for step in range(chips):
            target = lax.rem(chip + step, chips)
            core_out[column, target] = sums[band(target * 2 + 1 - core), :].astype(jnp.bfloat16)
            own[column, step] = sums[band(target * 2 + core), :]
        fold_copy(column).start()

    def fold(column):
        fold_copy(column).wait_recv()
        for step in range(1, chips):
            target = lax.rem(chip + step, chips)
            chip_out[column, step] = (
                own[column, step] + core_in[column, target].astype(jnp.float32)
            ).astype(jnp.bfloat16)
            chip_copy(step, column).start()
        own[column, 0] = own[column, 0] + core_in[column, chip].astype(jnp.float32)

    def column_step(column, carry):
        multiply(column)

        @pl.when(column > 0)
        def _():
            fold(column - 1)

        return carry

    lax.fori_loop(0, NIBBLES, column_step, 0)
    fold(NIBBLES - 1)

    factor = 1.0 / (45.0 * math.sqrt(groups * width))
    squares = jnp.zeros((part, 1), jnp.float32)
    for column in range(NIBBLES):
        span = slice(column * word_cols, (column + 1) * word_cols)
        total = own[column, 0]
        for step in range(1, chips):
            chip_copy(step, column).wait_recv()
            total += chip_in[column, step].astype(jnp.float32)
        fresh = (residual[:, span].astype(jnp.float32) + total * factor).astype(jnp.bfloat16)
        new_residual[:, span] = fresh
        values = fresh.astype(jnp.float32)
        squares += jnp.sum(values * values, axis=1, keepdims=True)
    inverse = lax.rsqrt(squares * (1.0 / (NIBBLES * word_cols)) + 1e-05)
    for column in range(NIBBLES):
        span = slice(column * word_cols, (column + 1) * word_cols)
        normed[:, span] = (new_residual[:, span].astype(jnp.float32) * inverse).astype(jnp.bfloat16)

    def drain_rows(piece, carry):
        for step in range(1, chips):
            peer_copy(step, piece).wait_send()
        for step in range(chips):
            core_copy(step, piece).wait_send()
        return carry

    lax.fori_loop(0, groups, drain_rows, 0)

    def drain_columns(column, carry):
        fold_copy(column).wait_send()
        for step in range(1, chips):
            chip_copy(step, column).wait_send()
        return carry

    lax.fori_loop(0, NIBBLES, drain_columns, 0)


def local(groups, hidden, signs, packed, group_scales, residual):
    rows, width = hidden.shape
    part = rows // groups
    chips = groups // 2
    word_cols = packed.shape[1]
    block = math.lcm(PALEY, LANES)
    table = np.kron(sylvester(block // PALEY), paley_table()).astype(ml_dtypes.bfloat16)
    signed = hidden * (2 * signs - 1).astype(jnp.bfloat16)[None, :]
    vmem = pl.BlockSpec(memory_space=pltpu.VMEM)
    anywhere = pl.BlockSpec(memory_space=pl.ANY)
    dma = pltpu.SemaphoreType.DMA
    tall = (NIBBLES, chips, part, word_cols)
    return pl.pallas_call(
        functools.partial(kernel, groups),
        out_shape=(
            jax.ShapeDtypeStruct(residual.shape, jnp.bfloat16),
            jax.ShapeDtypeStruct(residual.shape, jnp.bfloat16),
        ),
        in_specs=[anywhere, anywhere, vmem, anywhere, vmem],
        out_specs=(vmem, vmem),
        scratch_shapes=[
            pltpu.VMEM(packed.shape, jnp.int32),
            pltpu.VMEM((block, block), jnp.bfloat16),
            pltpu.VMEM((groups, rows, width), jnp.bfloat16),
            pltpu.VMEM(group_scales.shape, jnp.float32),
            pltpu.VMEM((NIBBLES, width, word_cols), jnp.bfloat16),
            pltpu.VMEM((rows, width), jnp.bfloat16),
            pltpu.VMEM((rows, word_cols), jnp.float32),
            pltpu.VMEM(tall, jnp.float32),
            pltpu.VMEM(tall, jnp.bfloat16),
            pltpu.VMEM(tall, jnp.bfloat16),
            pltpu.VMEM(tall, jnp.bfloat16),
            pltpu.VMEM(tall, jnp.bfloat16),
            dma,
            dma,
            dma,
            dma((chips, groups)),
            dma((chips, groups)),
            dma((chips, groups)),
            dma((chips, groups)),
            dma((NIBBLES,)),
            dma((NIBBLES,)),
            dma((chips, NIBBLES)),
            dma((chips, NIBBLES)),
        ],
        compiler_params=pltpu.CompilerParams(
            collective_id=0, has_side_effects=True, vmem_limit_bytes=67043328
        ),
    )(signed, packed, group_scales, jnp.asarray(table), residual)


def solution(mesh):
    return jax.shard_map(
        functools.partial(local, mesh.shape["tensor"]),
        mesh=mesh,
        in_specs=(
            P("dp", "tensor"),
            P("tensor"),
            P("tensor", None),
            P("tensor", None),
            P(("dp", "tensor"), None),
        ),
        out_specs=(P(("dp", "tensor"), None), P(("dp", "tensor"), None)),
        check_vma=False,
    )
```

time: 433 us -> 74 us (0.17)
  local copies, waits for them, and re-layouts: 235 us -> 3.74 us
  waiting for transfers between devices: 78.3 us -> 0 us
  Pallas kernels: 0 us -> 65.7 us
  other arithmetic: 54.8 us -> 3.61 us
  matrix products: 40.9 us -> 0 us
  between operations: 14.1 us -> 0.64 us
  starting transfers between devices: 8.93 us -> 0 us
    convert_element_type x2 -> x0, local copies, waits for them, and re-layouts: 216 us -> none  [the longest x1 215 us: local(): table = (outer[:, None, :, None] * inner[None, :, None, :]).reshape(local...]
    pallas_call x0 -> x1, Pallas kernels: none -> 65.7 us  [local(): pl.pallas_call(functools.partial(kernel, groups), out_shape=(jax.ShapeDty...]
    convert_element_type x5 -> x1, other arithmetic: 53.2 us -> 0.72 us  [local(): signed = hidden * (2 * signs - 1).astype(jnp.bfloat16)[None, :]]
    reduce_scatter x1 -> x0, waiting for transfers between devices: 45.6 us -> none  [local(): lax.psum_scatter(jnp.dot(rotated, weights, preferred_element_type=jnp.flo...]
    dot_general x3 -> x0, matrix products: 40.9 us -> none  [the longest x1 15.6 us: local(): jnp.dot(rotated, weights, preferred_element_type=jnp.float32)]
    all_to_all x2 -> x0, waiting for transfers between devices: 32.6 us -> none  [the longest x1 18.6 us: local(): lax.all_to_all(partial_rot, 'tensor', split_axis=0, concat_axis=1, tiled=...]
    unnamed x19 -> x2, local copies, waits for them, and re-layouts: 17 us -> 3.74 us
    all_to_all x2 -> x0, starting transfers between devices: 8.67 us -> none  [the longest x1 5.08 us: local(): lax.all_to_all(partial_rot, 'tensor', split_axis=0, concat_axis=1, tiled=...]
  transfers between devices with their start and end apart: 3 -> 0, of which waited for: 3 -> 0; matrix products, arithmetic and copies ran while one was open for 8% -> 0% of each run, Pallas kernels for 0% -> 0%
where the time goes in v1:
time: 74 us; the launch traced here: 73.7 us
  Pallas kernels  65.7 us (89%)
  local copies, waits for them, and re-layouts  3.74 us (5%)
  other arithmetic  3.61 us (5%)
    pallas_call x1, Pallas kernels, local(): pl.pallas_call(functools.partial(kernel, groups), out_shape=(jax.ShapeDty...  65.7 us
    unnamed x2, local copies, waits for them, and re-layouts  3.74 us
    mul x1, other arithmetic, local(): signed = hidden * (2 * signs - 1).astype(jnp.bfloat16)[None, :]  2.89 us

profile of v1, /device:TPU:0, one launch (start us, length us, event | category | flops | bytes accessed | tf_op | source)
XLA Modules:
  0.0 73.7 jit_solution(16601932585987844788)
XLA Ops:
  0.6 0.7 add_convert_fusion
  1.4 2.9 %broadcast_multiply_fusion.signed = bf16[256,3584]{1,0:T(8,128)(2,1)} fusion(bf16[256,3584]{1,0:T(8,128)(2,1)} %param.6, bf16[3584]{0:T(1024)(128)(2,1)S(1)} %add_convert_fusion), kind=kLoop, calls=%fused_computation | loop fusion | flops 917504 | bytes 3677184 | tf_op jit(solution)/shard_map/mul | solution.py:283
  4.2 65.7 %shard_map.77 = (bf16[64,4096]{1,0:T(8,128)(2,1)}, bf16[64,4096]{1,0:T(8,128)(2,1)}) custom-call(bf16[256,3584]{1,0:T(8,128)(2,1)} %broadcast_multiply_fusion.signed, s32[3584,512]{1,0:T(8,128)} %packed.1, s32[28,4096]{1,0:T(8,128)} %scales.1, bf16[896,896]{1,0:T(8,128)(2,1)} %constant.7.clone.table, bf16[64,4096]{1,0:T(8,128)(2,1)} %residual.1), custom_call_target="tpu_custom_call" | custom-call | tf_op jit(solution)/shard_map/pallas_call | solution.py:288
  70.0 1.9 %copy.10 = bf16[64,4096]{1,0:T(8,128)(2,1)} copy(bf16[64,4096]{1,0:T(8,128)(2,1)} %get-tuple-element.4) | data formatting | bytes 1048576
  71.9 1.9 %copy.11 = bf16[64,4096]{1,0:T(8,128)(2,1)} copy(bf16[64,4096]{1,0:T(8,128)(2,1)} %get-tuple-element.5) | data formatting | bytes 1048576

commit v2 on v1

v2 whole, which is shorter than its diff:
```python
import functools
import math

import jax
import jax.numpy as jnp
import ml_dtypes
import numpy as np
from jax import lax
from jax.experimental import pallas as pl
from jax.experimental.pallas import tpu as pltpu
from jax.sharding import PartitionSpec as P

PALEY = 28
LANES = 128
NIBBLES = 8
SLAB = 16
WAVES = 2
MESH = pl.DeviceIdType.MESH


def paley_table():
    offsets = (np.arange(13)[None, :] - np.arange(13)[:, None]) % 13
    residues = np.zeros(13)
    residues[np.arange(1, 13) ** 2 % 13] = 1.0
    quadratic = np.where(offsets == 0, 0.0, np.where(residues[offsets] > 0, 1.0, -1.0))
    conference = np.zeros((14, 14))
    conference[0, 1:] = 1.0
    conference[1:, 0] = 1.0
    conference[1:, 1:] = quadratic
    upper = np.array([[1.0, 1.0], [1.0, -1.0]])
    lower = np.array([[1.0, -1.0], [-1.0, -1.0]])
    return np.kron(conference, upper) + np.kron(np.eye(14), lower)


def sylvester(order):
    table = np.ones((1, 1))
    while table.shape[0] < order:
        table = np.kron(np.array([[1.0, 1.0], [1.0, -1.0]]), table)
    return table


def parity_sign(index, other, bits):
    common = index & other
    parity = common & 1
    for bit in range(1, bits):
        parity = parity ^ ((common >> bit) & 1)
    return (1 - 2 * parity).astype(jnp.float32)


def kernel(
    groups,
    waves,
    hidden,
    signs,
    packed,
    scales,
    table,
    residual,
    new_residual,
    words,
    inner,
    gathered,
    bits_in,
    flips,
    scale_f32,
    weights,
    rotated,
    sums,
    own,
    core_out,
    core_in,
    chip_out,
    chip_in,
    word_sem,
    inner_sem,
    self_sem,
    sign_send,
    sign_recv,
    peer_send,
    peer_recv,
    core_send,
    core_recv,
    fold_send,
    fold_recv,
    chip_send,
    chip_recv,
):
    me = lax.axis_index("tensor")
    chips = groups // 2
    chip, core = me // 2, lax.rem(me, 2)
    partner = chip * 2 + 1 - core
    part, width = hidden.shape[1:]
    sub = part // waves
    units = groups // waves
    group_count = scales.shape[0]
    group_size = width // group_count
    word_cols = packed.shape[1]
    block = table.shape[0]
    blocks = width // block
    bits = max(groups.bit_length() - 1, 1)

    word_copies = [
        pltpu.make_async_copy(packed, words, word_sem),
        pltpu.make_async_copy(table, inner, inner_sem),
        pltpu.make_async_copy(hidden, gathered.at[me], self_sem),
    ]
    for copy in word_copies:
        copy.start()

    def peer(step):
        return lax.rem(chip + step, chips) * 2 + core

    barrier = pltpu.get_barrier_semaphore()
    for step in range(1, groups):
        other = lax.rem(me + step, groups)
        pl.semaphore_signal(barrier, inc=1, device_id={"tensor": other}, device_id_type=MESH)
    pl.semaphore_wait(barrier, groups - 1)

    def sign_copy(step):
        return pltpu.make_async_remote_copy(
            src_ref=signs,
            dst_ref=bits_in.at[me],
            send_sem=sign_send.at[step],
            recv_sem=sign_recv.at[step],
            device_id={"tensor": lax.rem(me + step, groups)},
            device_id_type=MESH,
        )

    def place_of(unit):
        return pl.ds(lax.rem(unit, units) * waves, waves), pl.ds(pl.multiple_of(unit // units * sub, sub), sub)

    def peer_copy(step, unit):
        return pltpu.make_async_remote_copy(
            src_ref=hidden.at[place_of(unit)],
            dst_ref=gathered.at[(me,) + place_of(unit)],
            send_sem=peer_send.at[step, unit],
            recv_sem=peer_recv.at[step, unit],
            device_id={"tensor": peer(step)},
            device_id_type=MESH,
        )

    def core_copy(step, unit):
        slot = me if step == 0 else peer(chips - step)
        source = hidden.at[place_of(unit)] if step == 0 else gathered.at[(slot,) + place_of(unit)]
        return pltpu.make_async_remote_copy(
            src_ref=source,
            dst_ref=gathered.at[(slot,) + place_of(unit)],
            send_sem=core_send.at[step, unit],
            recv_sem=core_recv.at[step, unit],
            device_id={"tensor": partner},
            device_id_type=MESH,
        )

    for step in range(1, groups):
        sign_copy(step).start()
    for unit in range(groups):
        for step in range(1, chips):
            peer_copy(step, unit).start()
        core_copy(0, unit).start()

    scale_f32[...] = scales[...].astype(jnp.float32)
    word_copies[0].wait()

    def dequantize(index, carry):
        start = pl.multiple_of(index * SLAB, SLAB)
        group = index // (group_size // SLAB)
        values = words[pl.ds(start, SLAB), :] ^ jnp.int32(-2004318072)
        for nibble in range(NIBBLES):
            codes = lax.shift_right_arithmetic(lax.shift_left(values, 28 - 4 * nibble), 28)
            scale = scale_f32[pl.ds(group, 1), nibble * word_cols : (nibble + 1) * word_cols]
            weights[nibble, pl.ds(start, SLAB), :] = (codes.astype(jnp.float32) * scale).astype(jnp.bfloat16)
        return carry

    lax.fori_loop(0, width // SLAB, dequantize, 0)
    word_copies[1].wait()
    word_copies[2].wait()
    for step in range(1, groups):
        sign_copy(step).wait_recv()
    for step in range(groups):
        device = lax.rem(me + step, groups)
        source = signs if step == 0 else bits_in.at[device]
        flips[device] = (2 * source[...] - 1).astype(jnp.float32) * parity_sign(me, device, bits)

    scale_unit = 1.0 / math.sqrt(groups * width)

    def rotate(unit, carry):
        for step in range(1, chips):
            peer_copy(step, unit).wait_recv()
            core_copy(step, unit).start()
        for step in range(chips):
            core_copy(step, unit).wait_recv()
        mixed = []
        for place in range(blocks):
            total = jnp.zeros((part, block), jnp.float32)
            for device in range(groups):
                piece = gathered[(device,) + place_of(unit) + (pl.ds(place * block, block),)]
                first_row = place * block // LANES
                flip = jnp.concatenate(
                    [flips[device, pl.ds(first_row + i, 1), :] for i in range(block // LANES)], axis=1
                )
                total += piece.reshape(part, block).astype(jnp.float32) * flip
            high = total.astype(jnp.bfloat16)
            low = (total - high.astype(jnp.float32)).astype(jnp.bfloat16)
            both = jnp.dot(jnp.concatenate([high, low], axis=0), inner[...], preferred_element_type=jnp.float32)
            mixed.append(both[:part] + both[part:])
        stride = 1
        while stride < blocks:
            for low_index in range(blocks):
                if low_index & stride == 0:
                    first, second = mixed[low_index], mixed[low_index + stride]
                    mixed[low_index], mixed[low_index + stride] = first + second, first - second
            stride *= 2
        for place in range(blocks):
            rotated[unit // units, pl.ds(pl.multiple_of(lax.rem(unit, units) * part, part), part), place * block : (place + 1) * block] = (
                mixed[place] * scale_unit
            ).astype(jnp.bfloat16)
        return carry

    def band(index):
        return pl.ds(pl.multiple_of(index * sub, sub), sub)

    def fold_copy(column):
        return pltpu.make_async_remote_copy(
            src_ref=core_out.at[column],
            dst_ref=core_in.at[column],
            send_sem=fold_send.at[column],
            recv_sem=fold_recv.at[column],
            device_id={"tensor": partner},
            device_id_type=MESH,
        )

    def chip_copy(step, column):
        return pltpu.make_async_remote_copy(
            src_ref=chip_out.at[column, step],
            dst_ref=chip_in.at[column, step],
            send_sem=chip_send.at[step, column],
            recv_sem=chip_recv.at[step, column],
            device_id={"tensor": peer(step)},
            device_id_type=MESH,
        )

    def multiply(column):
        wave, nibble = column // NIBBLES, lax.rem(column, NIBBLES)
        sums[...] = jnp.dot(rotated[wave], weights[nibble], preferred_element_type=jnp.float32)
        for step in range(chips):
            target = lax.rem(chip + step, chips)
            core_out[column, target] = sums[band(target * 2 + 1 - core), :].astype(jnp.bfloat16)
            own[column, step] = sums[band(target * 2 + core), :]
        fold_copy(column).start()

    def fold(column):
        fold_copy(column).wait_recv()
        for step in range(1, chips):
            target = lax.rem(chip + step, chips)
            chip_out[column, step] = (
                own[column, step] + core_in[column, target].astype(jnp.float32)
            ).astype(jnp.bfloat16)
            chip_copy(step, column).start()
        own[column, 0] = own[column, 0] + core_in[column, chip].astype(jnp.float32)

    def column_step(column, carry):
        multiply(column)

        @pl.when(column > 0)
        def _():
            fold(column - 1)

        return carry

    for wave in range(waves):
        lax.fori_loop(wave * units, (wave + 1) * units, rotate, 0)
        lax.fori_loop(wave * NIBBLES, (wave + 1) * NIBBLES, column_step, 0)
    fold(waves * NIBBLES - 1)

    factor = 1.0 / (45.0 * math.sqrt(groups * width))
    for column in range(waves * NIBBLES):
        wave, nibble = column // NIBBLES, column % NIBBLES
        span = (slice(wave * sub, (wave + 1) * sub), slice(nibble * word_cols, (nibble + 1) * word_cols))
        total = own[column, 0]
        for step in range(1, chips):
            chip_copy(step, column).wait_recv()
            total += chip_in[column, step].astype(jnp.float32)
        new_residual[span] = (residual[span].astype(jnp.float32) + total * factor).astype(jnp.bfloat16)

    def drain_rows(unit, carry):
        for step in range(1, chips):
            peer_copy(step, unit).wait_send()
        for step in range(chips):
            core_copy(step, unit).wait_send()
        return carry

    for step in range(1, groups):
        sign_copy(step).wait_send()
    lax.fori_loop(0, groups, drain_rows, 0)

    def drain_columns(column, carry):
        fold_copy(column).wait_send()
        for step in range(1, chips):
            chip_copy(step, column).wait_send()
        return carry

    lax.fori_loop(0, waves * NIBBLES, drain_columns, 0)


def finish(fresh, new_residual, normed):
    values = fresh[...].astype(jnp.float32)
    new_residual[...] = fresh[...]
    inverse = lax.rsqrt(jnp.mean(values * values, axis=1, keepdims=True) + 1e-05)
    normed[...] = (values * inverse).astype(jnp.bfloat16)


def local(groups, hidden, signs, packed, group_scales, residual):
    rows, width = hidden.shape
    part = rows // groups
    chips = groups // 2
    waves = max(1, min(WAVES, part // SLAB, groups))
    word_cols = packed.shape[1]
    block = math.lcm(PALEY, LANES)
    table = np.kron(sylvester(block // PALEY), paley_table()).astype(ml_dtypes.bfloat16)
    vmem = pl.BlockSpec(memory_space=pltpu.VMEM)
    anywhere = pl.BlockSpec(memory_space=pl.ANY)
    dma = pltpu.SemaphoreType.DMA
    count = waves * NIBBLES
    tall = (count, chips, part // waves, word_cols)
    sign_shape = (width // LANES, LANES)
    out = jax.ShapeDtypeStruct(residual.shape, jnp.bfloat16)
    fresh = pl.pallas_call(
        functools.partial(kernel, groups, waves),
        out_shape=out,
        in_specs=[anywhere, vmem, anywhere, vmem, anywhere, vmem],
        out_specs=vmem,
        scratch_shapes=[
            pltpu.VMEM(packed.shape, jnp.int32),
            pltpu.VMEM((block, block), jnp.bfloat16),
            pltpu.VMEM((groups, groups, part, width), jnp.bfloat16),
            pltpu.VMEM((groups,) + sign_shape, jnp.int32),
            pltpu.VMEM((groups,) + sign_shape, jnp.float32),
            pltpu.VMEM(group_scales.shape, jnp.float32),
            pltpu.VMEM((NIBBLES, width, word_cols), jnp.bfloat16),
            pltpu.VMEM((waves, rows // waves, width), jnp.bfloat16),
            pltpu.VMEM((rows // waves, word_cols), jnp.float32),
            pltpu.VMEM(tall, jnp.float32),
            pltpu.VMEM(tall, jnp.bfloat16),
            pltpu.VMEM(tall, jnp.bfloat16),
            pltpu.VMEM(tall, jnp.bfloat16),
            pltpu.VMEM(tall, jnp.bfloat16),
            dma,
            dma,
            dma,
            dma((groups,)),
            dma((groups,)),
            dma((chips, groups)),
            dma((chips, groups)),
            dma((chips, groups)),
            dma((chips, groups)),
            dma((count,)),
            dma((count,)),
            dma((chips, count)),
            dma((chips, count)),
        ],
        compiler_params=pltpu.CompilerParams(
            collective_id=0, has_side_effects=True, vmem_limit_bytes=67043328
        ),
    )(
        hidden.reshape(groups, part, width),
        signs.reshape(sign_shape),
        packed,
        group_scales,
        jnp.asarray(table),
        residual,
    )
    return pl.pallas_call(
        finish,
        out_shape=(out, out),
        in_specs=[vmem],
        out_specs=(vmem, vmem),
    )(fresh)


def solution(mesh):
    return jax.shard_map(
        functools.partial(local, mesh.shape["tensor"]),
        mesh=mesh,
        in_specs=(
            P("dp", "tensor"),
            P("tensor"),
            P("tensor", None),
            P("tensor", None),
            P(("dp", "tensor"), None),
        ),
        out_specs=(P(("dp", "tensor"), None), P(("dp", "tensor"), None)),
        check_vma=False,
    )
```

time: 74 us -> 65 us (0.88)
  local copies, waits for them, and re-layouts: 3.74 us -> 0 us
  other arithmetic: 3.61 us -> 0 us
  Pallas kernels: 65.7 us -> 64.2 us
    unnamed x2 -> x0, local copies, waits for them, and re-layouts: 3.74 us -> none
    mul x1 -> x0, other arithmetic: 2.89 us -> none  [local(): signed = hidden * (2 * signs - 1).astype(jnp.bfloat16)[None, :]]
    pallas_call x1 -> x2, Pallas kernels: 65.7 us -> 64.2 us  [the longest x1 62.1 us: local(): pl.pallas_call(functools.partial(kernel, groups, waves), out_shape=out, i...]
where the time goes in v2:
time: 65 us; the launch traced here: 64.8 us
  Pallas kernels  64.2 us (99%)
    pallas_call x1, Pallas kernels, local(): pl.pallas_call(functools.partial(kernel, groups, waves), out_shape=out, i...  62.1 us
    pallas_call x1, Pallas kernels, local(): pl.pallas_call(finish, out_shape=(out, out), in_specs=[vmem], out_specs=(...  2.08 us

profile of v2, /device:TPU:0, one launch (start us, length us, event | category | flops | bytes accessed | tf_op | source)
XLA Modules:
  0.0 64.8 jit_solution(2418013711352090045)
XLA Ops:
  0.6 62.1 %shard_map.77.fresh = bf16[64,4096]{1,0:T(8,128)(2,1)} custom-call(bf16[4,64,3584]{2,1,0:T(8,128)(2,1)} %bitcast.2, s32[28,128]{1,0:T(8,128)} %bitcast.3, s32[3584,512]{1,0:T(8,128)} %packed.1, s32[28,4096]{1,0:T(8,128)} %scales.1, bf16[896,896]{1,0:T(8,128)(2,1)} %constant.2.clone.table, bf16[64,4096]{1,0:T(8,128)(2,1)} %residual.1), custom_call_target="tpu_custom_call" | custom-call | tf_op jit(solution)/shard_map/pallas_call | solution.py:327
  62.7 2.1 %shard_map.78 = (bf16[64,4096]{1,0:T(8,128)(2,1)}, bf16[64,4096]{1,0:T(8,128)(2,1)}) custom-call(bf16[64,4096]{1,0:T(8,128)(2,1)} %shard_map.77.fresh), custom_call_target="tpu_custom_call" | custom-call | tf_op jit(solution)/shard_map/pallas_call | solution.py:372

commit v3 on v2

--- a/solution.py
+++ b/solution.py
@@ -53,10 +53,12 @@
     hidden,
     signs,
     packed,
+    scales_any,
+    table,
+    residual_any,
+    new_residual,
     scales,
-    table,
     residual,
-    new_residual,
     words,
     inner,
     gathered,
@@ -74,6 +76,9 @@
     word_sem,
     inner_sem,
     self_sem,
+    flip_sem,
+    scale_sem,
+    residual_sem,
     sign_send,
     sign_recv,
     peer_send,
@@ -103,10 +108,10 @@
         pltpu.make_async_copy(packed, words, word_sem),
         pltpu.make_async_copy(table, inner, inner_sem),
         pltpu.make_async_copy(hidden, gathered.at[me], self_sem),
+        pltpu.make_async_copy(signs, bits_in.at[me], flip_sem),
+        pltpu.make_async_copy(scales_any, scales, scale_sem),
+        pltpu.make_async_copy(residual_any, residual, residual_sem),
     ]
-    for copy in word_copies:
-        copy.start()
-
     def peer(step):
         return lax.rem(chip + step, chips) * 2 + core
 
@@ -158,6 +163,10 @@
             peer_copy(step, unit).start()
         core_copy(0, unit).start()
 
+    for copy in word_copies:
+        copy.start()
+
+    word_copies[4].wait()
     scale_f32[...] = scales[...].astype(jnp.float32)
     word_copies[0].wait()
 
@@ -174,12 +183,13 @@
     lax.fori_loop(0, width // SLAB, dequantize, 0)
     word_copies[1].wait()
     word_copies[2].wait()
+    word_copies[3].wait()
+    word_copies[5].wait()
     for step in range(1, groups):
         sign_copy(step).wait_recv()
     for step in range(groups):
         device = lax.rem(me + step, groups)
-        source = signs if step == 0 else bits_in.at[device]
-        flips[device] = (2 * source[...] - 1).astype(jnp.float32) * parity_sign(me, device, bits)
+        flips[device] = (2 * bits_in[device] - 1).astype(jnp.float32) * parity_sign(me, device, bits)
 
     scale_unit = 1.0 / math.sqrt(groups * width)
 
@@ -327,9 +337,11 @@
     fresh = pl.pallas_call(
         functools.partial(kernel, groups, waves),
         out_shape=out,
-        in_specs=[anywhere, vmem, anywhere, vmem, anywhere, vmem],
+        in_specs=[anywhere] * 6,
         out_specs=vmem,
         scratch_shapes=[
+            pltpu.VMEM(group_scales.shape, jnp.int32),
+            pltpu.VMEM(residual.shape, jnp.bfloat16),
             pltpu.VMEM(packed.shape, jnp.int32),
             pltpu.VMEM((block, block), jnp.bfloat16),
             pltpu.VMEM((groups, groups, part, width), jnp.bfloat16),
@@ -344,6 +356,9 @@
             pltpu.VMEM(tall, jnp.bfloat16),
             pltpu.VMEM(tall, jnp.bfloat16),
             pltpu.VMEM(tall, jnp.bfloat16),
+            dma,
+            dma,
+            dma,
             dma,
             dma,
             dma,

time: 65 us -> 64 us (0.985)
  Pallas kernels: 64.2 us -> 63.2 us
    pallas_call x1, Pallas kernels: 62.1 us -> 61.2 us  [local(): pl.pallas_call(functools.partial(kernel, groups, waves), out_shape=out, i...]
where the time goes in v3:
time: 64 us; the launch traced here: 63.9 us
  Pallas kernels  63.2 us (99%)
  between operations  0.64 us (1%)
    pallas_call x1, Pallas kernels, local(): pl.pallas_call(functools.partial(kernel, groups, waves), out_shape=out, i...  61.2 us
    pallas_call x1, Pallas kernels, local(): pl.pallas_call(finish, out_shape=(out, out), in_specs=[vmem], out_specs=(...  2.08 us

profile of v3, /device:TPU:0, one launch (start us, length us, event | category | flops | bytes accessed | tf_op | source)
XLA Modules:
  0.0 63.9 jit_solution(14852819765366699332)
XLA Ops:
  0.6 61.2 %shard_map.77.fresh = bf16[64,4096]{1,0:T(8,128)(2,1)} custom-call(bf16[4,64,3584]{2,1,0:T(8,128)(2,1)} %bitcast.2, s32[28,128]{1,0:T(8,128)} %bitcast.3, s32[3584,512]{1,0:T(8,128)} %packed.1, s32[28,4096]{1,0:T(8,128)} %scales_any.1, bf16[896,896]{1,0:T(8,128)(2,1)} %constant.2.clone.table, bf16[64,4096]{1,0:T(8,128)(2,1)} %residual_any.1), custom_call_target="tpu_custom_call" | custom-call | tf_op jit(solution)/shard_map/pallas_call | solution.py:337
  61.8 2.1 %shard_map.78 = (bf16[64,4096]{1,0:T(8,128)(2,1)}, bf16[64,4096]{1,0:T(8,128)(2,1)}) custom-call(bf16[64,4096]{1,0:T(8,128)(2,1)} %shard_map.77.fresh), custom_call_target="tpu_custom_call" | custom-call | tf_op jit(solution)/shard_map/pallas_call | solution.py:387
